TPU v7x, 32 devices: a whole 2x2x4 slice. The times are simulated.
32 devices in a mesh: row: 8 (over y, x, core), col: 4 (over z).
Axes of the slice: x: 2, y: 2, z: 4, core: 2. Of those that a mesh axis runs over, the one named last changes fastest.
Arguments:
- covariance: bfloat16 [16384, 16384], P('row', 'col'), may hold values from -0.12 to 0.6, as said below
- estimate: bfloat16 [16384, 16384], P('row', 'col'), may hold values from -2.3 to 12, as said below
- dual_var: bfloat16 [16384, 16384], P('row', 'col'), may hold values from -1.7 to 1.7, as said below
- start_basis: float32 [16384, 128], P('row'), may hold values from -6 to 6
Outputs:
- next_estimate: float32 [16384, 16384], P('row', 'col')
- next_dual: bfloat16 [16384, 16384], P('row', 'col')
Inputs may be any that keep to these rules, and one draw needn't show every extreme that they name: `covariance`: symmetric. `estimate`: symmetric. `dual_var`: symmetric.
All inputs are finite; a program needn't handle non-finite values.
Results may differ from a plain program's by a relative error of at most 0.001.
Values sent between devices are 32-bit elements; how exact they have to be, the bound alone decides.
A program may use at most 192 MiB of HBM per device.

v0:
```python
import functools

import jax
import jax.numpy as jnp
from jax import lax
from jax.experimental import pallas as pl
from jax.experimental.pallas import tpu as pltpu
from jax.sharding import PartitionSpec as P

NS_ITERS = 12


penalty = 0.01
threshold = 0.2
base_level = 10.0
highest = lax.Precision.HIGHEST


def from_root(value, axis, source):
    kept = jnp.where(lax.axis_index(axis) == source, value, 0).astype(value.dtype)
    return lax.psum(kept, axis)


def inner_product(left_side, right_side):
    return lax.dot_general(
        left_side,
        right_side,
        (((0,), (0,)), ((), ())),
        precision=highest,
        preferred_element_type=jnp.float32,
    )


def normalize(mapped, gram_matrix):
    lower_factor = jnp.linalg.cholesky(gram_matrix)
    identity = jnp.eye(gram_matrix.shape[0], dtype=jnp.float32)
    inverse = lax.linalg.triangular_solve(lower_factor, identity, left_side=True, lower=True)
    return jnp.dot(mapped, inverse.T, precision=highest, preferred_element_type=jnp.float32)


def response_of(ritz_matrix):
    identity = jnp.eye(ritz_matrix.shape[0], dtype=jnp.float32)
    square = (
        jnp.dot(ritz_matrix, ritz_matrix, precision=highest, preferred_element_type=jnp.float32)
        + 4.0 * penalty * identity
    )
    frobenius = jnp.sqrt(jnp.sum(square * square))

    def newton(sweep_index, state_pair):
        iterate, partner = state_pair
        factor = 0.5 * (
            3.0 * identity
            - jnp.dot(partner, iterate, precision=highest, preferred_element_type=jnp.float32)
        )
        return (
            jnp.dot(iterate, factor, precision=highest, preferred_element_type=jnp.float32),
            jnp.dot(factor, partner, precision=highest, preferred_element_type=jnp.float32),
        )

    iterate, partner = lax.fori_loop(0, NS_ITERS, newton, (square / frobenius, identity))
    square_root = jnp.sqrt(frobenius) * iterate
    return (ritz_matrix + square_root) / (2.0 * penalty) - base_level * identity


def column_basis(shifted, row_basis):
    partial_terms = lax.dot_general(
        shifted,
        row_basis,
        (((0,), (0,)), ((), ())),
        precision=highest,
        preferred_element_type=jnp.float32,
    )
    mapped = lax.psum(partial_terms, "row")
    gram_matrix = lax.psum(inner_product(mapped, mapped), "col")
    return normalize(mapped, gram_matrix)


def row_image(shifted, col_basis):
    local_terms = jnp.dot(shifted, col_basis, precision=highest, preferred_element_type=jnp.float32)
    return lax.psum(local_terms, "col")


def row_inner(left_side, right_side):
    return lax.psum(inner_product(left_side, right_side), "row")


def plain_body(covariance, estimate, dual_var, start_basis):
    shifted = penalty * (
        estimate.astype(jnp.float32) - dual_var.astype(jnp.float32)
    ) - covariance.astype(jnp.float32)
    rows_tile = shifted.shape[0]
    cols_tile = shifted.shape[1]
    row_basis = start_basis
    col_basis = column_basis(shifted, row_basis)
    blocks_per_column = lax.axis_size("row") // lax.axis_size("col")
    row_index = lax.axis_index("row")
    own_block = lax.dynamic_slice_in_dim(
        col_basis, row_index % blocks_per_column * rows_tile, rows_tile, 0
    )
    row_basis = from_root(own_block, "col", row_index // blocks_per_column)
    product = row_image(shifted, col_basis)
    raw_ritz = row_inner(row_basis, product)
    ritz_matrix = 0.5 * (raw_ritz + raw_ritz.T)
    response = response_of(ritz_matrix)
    weighted = jnp.dot(row_basis, response, precision=highest, preferred_element_type=jnp.float32)
    theta_tile = lax.dot_general(
        weighted,
        col_basis,
        (((1,), (1,)), ((), ())),
        precision=highest,
        preferred_element_type=jnp.float32,
    )
    row_ids = row_index * rows_tile + lax.broadcasted_iota(jnp.int32, (rows_tile, 1), 0)
    col_ids = lax.axis_index("col") * cols_tile + lax.broadcasted_iota(jnp.int32, (1, cols_tile), 1)
    theta_tile = theta_tile + jnp.where(row_ids == col_ids, base_level, 0.0)
    mixture = theta_tile + dual_var.astype(jnp.float32)
    clipped = jnp.clip(mixture, -threshold, threshold)
    return (mixture - clipped, clipped.astype(jnp.bfloat16))


MESH = pl.DeviceIdType.MESH
VMEM = pl.BlockSpec(memory_space=pltpu.VMEM)
VMEM_BYTES = 60 * 1024 * 1024


def high_dot(left_side, right_side, dims):
    return lax.dot_general(
        left_side, right_side, (dims, ((), ())), precision=highest, preferred_element_type=jnp.float32
    )


def split(value):
    upper = value.astype(jnp.bfloat16)
    return upper, (value - upper.astype(jnp.float32)).astype(jnp.bfloat16)


def image_kernel(est_ref, dual_ref, cov_ref, basis_ref, out_ref, left_ref, acc_ref):
    blocks, both, depth = left_ref.shape
    half = both // 2

    @pl.when(pl.program_id(0) == 0)
    def _():
        for index in range(blocks):
            upper, lower = split(basis_ref[index * depth : (index + 1) * depth, :].T)
            left_ref[index, :half] = upper
            left_ref[index, half:] = lower

    acc_ref[...] = jnp.zeros_like(acc_ref)

    def step(block, carry):
        rows = pl.ds(pl.multiple_of(block * depth, depth), depth)
        shifted = penalty * (
            est_ref[rows, :].astype(jnp.float32) - dual_ref[rows, :].astype(jnp.float32)
        ) - cov_ref[rows, :].astype(jnp.float32)
        upper, lower = split(shifted)
        acc_ref[...] += jnp.dot(left_ref[block], upper, preferred_element_type=jnp.float32)
        acc_ref[:half] += jnp.dot(left_ref[block, :half], lower, preferred_element_type=jnp.float32)
        return carry

    lax.fori_loop(0, blocks, step, 0)
    out_ref[0] = acc_ref[:half] + acc_ref[half:]


def image_parts(matrices, start_basis, piece):
    rows_tile, cols_tile = matrices[0].shape
    rank = start_basis.shape[1]
    depth = min(256, rows_tile)
    return pl.pallas_call(
        image_kernel,
        grid=(cols_tile // piece,),
        in_specs=[pl.BlockSpec((rows_tile, piece), lambda step: (0, step))] * 3
        + [pl.BlockSpec(start_basis.shape, lambda step: (0, 0))],
        out_specs=pl.BlockSpec((1, rank, piece), lambda step: (step, 0, 0)),
        out_shape=jax.ShapeDtypeStruct((cols_tile // piece, rank, piece), jnp.float32),
        scratch_shapes=[
            pltpu.VMEM((rows_tile // depth, 2 * rank, depth), jnp.bfloat16),
            pltpu.VMEM((2 * rank, piece), jnp.float32),
        ],
        compiler_params=pltpu.CompilerParams(
            dimension_semantics=("arbitrary",), vmem_limit_bytes=VMEM_BYTES
        ),
    )(*matrices, start_basis)


def moment_kernel(est_ref, dual_ref, cov_ref, rows_ref, cols_ref, out_ref, right_ref):
    count, rank, piece = cols_ref.shape

    @pl.when(pl.program_id(0) == 0)
    def _():
        for k in range(count):
            flat = cols_ref[k].T
            scaled_upper, scaled_lower = split(penalty * flat)
            upper, lower = split(flat)
            right_ref[0, k, :, :rank] = scaled_upper
            right_ref[0, k, :, rank:] = scaled_lower
            right_ref[1, k, :, :rank] = -scaled_upper
            right_ref[1, k, :, rank:] = -scaled_lower
            right_ref[2, k, :, :rank] = -upper
            right_ref[2, k, :, rank:] = -lower
        own = cols_ref[lax.axis_index("row")]
        out_ref[:rank] = high_dot(own, own, ((1,), (1,)))
        out_ref[rank:] = jnp.zeros((rank, rank), jnp.float32)

    image = jnp.zeros((est_ref.shape[0], 2 * rank), jnp.float32)
    for k in range(count):
        where = slice(k * piece, (k + 1) * piece)
        for which, tile in enumerate((est_ref, dual_ref, cov_ref)):
            image += jnp.dot(tile[:, where], right_ref[which, k], preferred_element_type=jnp.float32)
    out_ref[rank:] += high_dot(rows_ref[0], image[:, :rank] + image[:, rank:], ((1,), (0,)))


def moment_terms(matrices, rows, cols):
    rows_tile, cols_tile = matrices[0].shape
    count, rank, piece = cols.shape
    depth = min(256, piece)
    per = piece // depth
    return pl.pallas_call(
        moment_kernel,
        grid=(rows_tile // depth,),
        in_specs=[pl.BlockSpec((depth, cols_tile), lambda step: (step, 0))] * 3
        + [
            pl.BlockSpec((1, rank, depth), lambda step: (step // per, 0, step % per)),
            pl.BlockSpec(cols.shape, lambda step: (0, 0, 0)),
        ],
        out_specs=pl.BlockSpec((2 * rank, rank), lambda step: (0, 0)),
        out_shape=jax.ShapeDtypeStruct((2 * rank, rank), jnp.float32),
        scratch_shapes=[pltpu.VMEM((3, count, piece, 2 * rank), jnp.bfloat16)],
        compiler_params=pltpu.CompilerParams(
            dimension_semantics=("arbitrary",), vmem_limit_bytes=VMEM_BYTES
        ),
    )(*matrices, rows, cols)


def spread_kernel(n_row, n_col, part_ref, mc_ref, mr_ref, near, other, zbuf, sems):
    row, col = lax.axis_index("row"), lax.axis_index("col")
    chips = n_row // 2
    chip, core = row // 2, row % 2
    sibling = chip * 2 + 1 - core
    ratio = n_row // n_col
    group = n_row // ratio

    barrier = pltpu.get_barrier_semaphore()

    def greet_row(t, carry):
        pl.semaphore_signal(barrier, inc=1, device_id=((row + t) % n_row, col), device_id_type=MESH)
        return carry

    def greet_col(t, carry):
        pl.semaphore_signal(barrier, inc=1, device_id=(row, (col + t) % n_col), device_id_type=MESH)
        return carry

    lax.fori_loop(1, n_row, greet_row, 0)
    lax.fori_loop(1, n_col, greet_col, 0)
    pl.semaphore_wait(barrier, n_row - 1 + n_col - 1)

    send1, recv1, send2, recv2, send3, recv3, send4, recv4, send5, recv5, send6, recv6 = sems

    def copy(src, dst, send, recv, target):
        return pltpu.make_async_remote_copy(
            src_ref=src, dst_ref=dst, send_sem=send, recv_sem=recv, device_id=target, device_id_type=MESH
        )

    first = []
    for t in range(chips):
        there = (chip + 1 + t) % chips
        first.append(
            copy(part_ref.at[2 * there + 1 - core], near.at[t], send1.at[t], recv1.at[t], (sibling, col))
        )
        first[-1].start()
    second = []
    for t in range(chips):
        there = (chip + 1 + t) % chips
        first[t].wait_recv()
        if t < chips - 1:
            near[t] = near[t] + part_ref[2 * there + core]
            second.append(
                copy(near.at[t], other.at[t], send2.at[t], recv2.at[t], (2 * there + core, col))
            )
            second[-1].start()
    total = near[chips - 1] + part_ref[row]
    for t in range(chips - 1):
        second[t].wait_recv()
        total += other[t]
    mc_ref[row] = total

    own = mc_ref.at[row]
    along = []
    for t in range(n_col - 1):
        along.append(copy(own, zbuf.at[t], send4.at[t], recv4.at[t], (row, (col + 1 + t) % n_col)))
        along[-1].start()
    plane = []
    for t in range(chips - 1):
        there = (chip + 1 + t) % chips
        plane.append(copy(own, own, send3.at[t], recv3.at[t], (2 * there + core, col)))
        plane[-1].start()
    pair = [copy(own, own, send5.at[0], recv5.at[0], (sibling, col))]
    pair[0].start()

    slot = row % group
    onward = []
    for t in range(n_col - 1):
        source = (col + n_col - 1 - t) % n_col
        target = source * ratio + row // group
        along[t].wait_recv()
        hop = copy(zbuf.at[t], mr_ref.at[slot], send6.at[t], recv6.at[slot], (target, col))

        @pl.when(target != row)
        def _():
            hop.start()

        @pl.when(target == row)
        def _():
            mr_ref[slot] = zbuf[t]

        onward.append((hop, target))

    for t in range(chips - 1):
        source = 2 * ((chip + chips - 1 - t) % chips) + core
        arrived = mc_ref.at[source]
        copy(own, arrived, send3.at[t], recv3.at[t], (row, col)).wait_recv()
        pair.append(copy(arrived, arrived, send5.at[t + 1], recv5.at[t + 1], (sibling, col)))
        pair[-1].start()
    for t in range(chips):
        source = 2 * ((chip + chips - t) % chips) + 1 - core
        copy(own, mc_ref.at[source], send5.at[t], recv5.at[t], (sibling, col)).wait_recv()

    @pl.when(row // ratio == col)
    def _():
        for k in range(group):
            mr_ref[k] = mc_ref[(row % ratio) * group + k]

    for k in range(group):
        @pl.when((row // ratio != col) & ((row % ratio) * group + k != row))
        def _():
            copy(zbuf.at[0], mr_ref.at[k], send6.at[0], recv6.at[k], (sibling, col)).wait_recv()

    for item in first + second + along + plane + pair:
        item.wait_send()
    for hop, target in onward:
        @pl.when(target != row)
        def _():
            hop.wait_send()


def spread(parts, n_row, n_col):
    rank, piece = parts.shape[1:]
    chips, ratio = n_row // 2, n_row // n_col
    group = n_row // ratio
    dma = pltpu.SemaphoreType.DMA

    def kernel(part_ref, mc_ref, mr_ref, near, other, zbuf, *sems):
        spread_kernel(n_row, n_col, part_ref, mc_ref, mr_ref, near, other, zbuf, sems)

    return pl.pallas_call(
        kernel,
        in_specs=[VMEM],
        out_specs=(VMEM, VMEM),
        out_shape=(
            jax.ShapeDtypeStruct((n_row, rank, piece), jnp.float32),
            jax.ShapeDtypeStruct((group, rank, piece), jnp.float32),
        ),
        scratch_shapes=[
            pltpu.VMEM((chips, rank, piece), jnp.float32),
            pltpu.VMEM((chips - 1, rank, piece), jnp.float32),
            pltpu.VMEM((n_col - 1, rank, piece), jnp.float32),
            dma((chips,)), dma((chips,)),
            dma((chips - 1,)), dma((chips - 1,)),
            dma((chips - 1,)), dma((chips - 1,)),
            dma((n_col - 1,)), dma((n_col - 1,)),
            dma((chips,)), dma((chips,)),
            dma((n_col - 1,)), dma((group,)),
        ],
        compiler_params=pltpu.CompilerParams(
            collective_id=0, has_side_effects=True, vmem_limit_bytes=VMEM_BYTES
        ),
    )(parts)


def total_kernel(n_row, n_col, term_ref, out_ref, terms, part, planes, *sems):
    send1, recv1, send2, recv2, send3, recv3 = sems
    row, col = lax.axis_index("row"), lax.axis_index("col")
    barrier = pltpu.get_barrier_semaphore()

    def greet_row(t, carry):
        pl.semaphore_signal(barrier, inc=1, device_id=((row + t) % n_row, col), device_id_type=MESH)
        return carry

    def greet_col(t, carry):
        pl.semaphore_signal(barrier, inc=1, device_id=(row, (col + t) % n_col), device_id_type=MESH)
        return carry

    lax.fori_loop(1, n_row, greet_row, 0)
    lax.fori_loop(1, n_col, greet_col, 0)
    pl.semaphore_wait(barrier, n_row - 1 + n_col - 1)

    def copy(src, dst, send, recv, target):
        return pltpu.make_async_remote_copy(
            src_ref=src, dst_ref=dst, send_sem=send, recv_sem=recv, device_id=target, device_id_type=MESH
        )

    first = []
    for t in range(1, n_row):
        there = (row + t) % n_row
        first.append(copy(term_ref.at[there], terms.at[t], send1.at[t], recv1.at[t], (there, col)))
        first[-1].start()
    summed = term_ref[row]
    for t in range(1, n_row):
        first[t - 1].wait_recv()
        summed += terms[t]
    part[...] = summed
    second = []
    for t in range(1, n_col):
        there = (col + t) % n_col
        second.append(copy(part, planes.at[col], send2.at[t], recv2.at[col], (row, there)))
        second[-1].start()
    planes[col] = summed
    for t in range(1, n_col):
        source = (col + t) % n_col
        copy(part, planes.at[source], send2.at[t], recv2.at[source], (row, source)).wait_recv()
    out_ref[row] = jnp.sum(planes[...], axis=0)
    third = []
    for t in range(1, n_row):
        there = (row + t) % n_row
        third.append(copy(out_ref.at[row], out_ref.at[row], send3.at[t], recv3.at[t], (there, col)))
        third[-1].start()
    for t in range(1, n_row):
        source = (row + n_row - t) % n_row
        copy(out_ref.at[row], out_ref.at[source], send3.at[t], recv3.at[t], (source, col)).wait_recv()
    for item in first + second + third:
        item.wait_send()


def total(terms, n_row, n_col):
    blocks = terms.reshape(n_row, terms.shape[0] // n_row, terms.shape[1])
    block = blocks.shape[1:]
    dma = pltpu.SemaphoreType.DMA
    summed = pl.pallas_call(
        functools.partial(total_kernel, n_row, n_col),
        in_specs=[VMEM],
        out_specs=VMEM,
        out_shape=jax.ShapeDtypeStruct(blocks.shape, jnp.float32),
        scratch_shapes=[
            pltpu.VMEM(blocks.shape, jnp.float32),
            pltpu.VMEM(block, jnp.float32),
            pltpu.VMEM((n_col, *block), jnp.float32),
            dma((n_row,)), dma((n_row,)),
            dma((n_col,)), dma((n_col,)),
            dma((n_row,)), dma((n_row,)),
        ],
        compiler_params=pltpu.CompilerParams(collective_id=1, has_side_effects=True),
    )(blocks)
    return summed.reshape(terms.shape)


def weight_kernel(moment_ref, rows_ref, out_ref, inverse_ref, ritz_ref, iterate_ref, partner_ref):
    rank = rows_ref.shape[1]
    row_ids = lax.broadcasted_iota(jnp.int32, (rank, rank), 0)
    col_ids = lax.broadcasted_iota(jnp.int32, (rank, rank), 1)
    line_ids = lax.broadcasted_iota(jnp.int32, (1, rank), 1)
    identity = jnp.where(row_ids == col_ids, 1.0, 0.0)
    inverse = moment_ref[:rank]
    for k in range(rank):
        pivot = 1.0 / inverse[k : k + 1, k : k + 1]
        column = inverse[:, k : k + 1]
        line = jnp.where(line_ids == k, 1.0, inverse[k : k + 1, :]) * pivot
        inverse = jnp.where(
            row_ids == k, line, jnp.where(col_ids == k, 0.0, inverse) - column * line
        )
    inverse_ref[...] = inverse
    raw = moment_ref[rank:]
    iterate_ref[...] = 0.5 * (raw + raw.T)
    plain = ((1,), (0,))
    ritz_ref[...] = high_dot(inverse_ref[...], iterate_ref[...], plain)
    square = high_dot(ritz_ref[...], ritz_ref[...], plain) + 4.0 * penalty * identity
    frobenius = jnp.sqrt(jnp.sum(square * square.T, keepdims=True))
    iterate_ref[...] = square / frobenius
    partner_ref[...] = identity

    def newton(step, carry):
        iterate, partner = iterate_ref[...], partner_ref[...]
        factor = 0.5 * (3.0 * identity - high_dot(partner, iterate, plain))
        iterate_ref[...] = high_dot(iterate, factor, plain)
        partner_ref[...] = high_dot(factor, partner, plain)
        return carry

    lax.fori_loop(0, NS_ITERS, newton, 0)
    root = jnp.sqrt(frobenius) * iterate_ref[...]
    response = (ritz_ref[...] + root) / (2.0 * penalty) - base_level * identity
    partner_ref[...] = high_dot(response, inverse_ref[...], plain)
    piece = rows_ref.shape[2]
    for k in range(rows_ref.shape[0]):
        out_ref[k * piece : (k + 1) * piece, :] = high_dot(rows_ref[k].T, partner_ref[...], plain)


def finish_kernel(weighted_ref, cols_ref, dual_ref, est_ref, clip_ref, right_ref, low_ref):
    step = pl.program_id(0)
    count, rank, piece = cols_ref.shape
    depth = dual_ref.shape[0]

    @pl.when(step == 0)
    def _():
        for k in range(count):
            upper, lower = split(cols_ref[k])
            right_ref[k, :rank] = upper
            right_ref[k, rank:] = upper
            low_ref[k] = lower

    upper, lower = split(weighted_ref[...])
    both = jnp.concatenate([upper, lower], axis=1)
    n_grid = pl.num_programs(0)
    row_start = (lax.axis_index("row") * n_grid + step) * depth
    gap = (
        lax.broadcasted_iota(jnp.int32, (depth, piece), 1)
        - lax.broadcasted_iota(jnp.int32, (depth, piece), 0)
    )
    for k in range(count):
        where = slice(k * piece, (k + 1) * piece)
        col_start = lax.axis_index("col") * (count * piece) + k * piece
        theta = jnp.dot(both, right_ref[k], preferred_element_type=jnp.float32)
        theta += jnp.dot(upper, low_ref[k], preferred_element_type=jnp.float32)
        theta += jnp.where(gap == row_start - col_start, base_level, 0.0)
        mixture = theta + dual_ref[:, where].astype(jnp.float32)
        clipped = jnp.clip(mixture, -threshold, threshold)
        est_ref[:, where] = mixture - clipped
        clip_ref[:, where] = clipped.astype(jnp.bfloat16)


def finish(weighted, cols, dual_var):
    rows_tile, cols_tile = dual_var.shape
    count, rank, piece = cols.shape
    depth = min(512, rows_tile)
    wide = pl.BlockSpec((depth, cols_tile), lambda step: (step, 0))
    return pl.pallas_call(
        finish_kernel,
        grid=(rows_tile // depth,),
        in_specs=[
            pl.BlockSpec((depth, rank), lambda step: (step, 0)),
            pl.BlockSpec(cols.shape, lambda step: (0, 0, 0)),
            wide,
        ],
        out_specs=(wide, wide),
        out_shape=(
            jax.ShapeDtypeStruct(dual_var.shape, jnp.float32),
            jax.ShapeDtypeStruct(dual_var.shape, jnp.bfloat16),
        ),
        scratch_shapes=[
            pltpu.VMEM((count, 2 * rank, piece), jnp.bfloat16),
            pltpu.VMEM((count, rank, piece), jnp.bfloat16),
        ],
        compiler_params=pltpu.CompilerParams(
            dimension_semantics=("arbitrary",), vmem_limit_bytes=VMEM_BYTES
        ),
    )(weighted, cols, dual_var)


def fast_body(n_row, n_col, covariance, estimate, dual_var, start_basis):
    rows_tile, cols_tile = covariance.shape
    rank = start_basis.shape[1]
    piece = cols_tile // n_row
    matrices = (estimate, dual_var, covariance)
    parts = image_parts(matrices, start_basis, piece)
    cols, rows = spread(parts, n_row, n_col)
    moments = moment_terms(matrices, rows, cols)
    moments = total(moments, n_row, n_col)
    weighted = pl.pallas_call(
        weight_kernel,
        in_specs=[VMEM, VMEM],
        out_specs=VMEM,
        out_shape=jax.ShapeDtypeStruct((rows_tile, rank), jnp.float32),
        scratch_shapes=[pltpu.VMEM((rank, rank), jnp.float32)] * 4,
        compiler_params=pltpu.CompilerParams(vmem_limit_bytes=VMEM_BYTES),
    )(moments, rows)
    return finish(weighted, cols, dual_var)


def body(covariance, estimate, dual_var, start_basis):
    n_row, n_col = lax.axis_size("row"), lax.axis_size("col")
    rows_tile, cols_tile = covariance.shape
    rank = start_basis.shape[1]
    piece = cols_tile // n_row
    fits = (
        n_row % 2 == 0
        and n_row % n_col == 0
        and cols_tile % n_row == 0
        and piece % 128 == 0
        and rows_tile % piece == 0
        and rank % 128 == 0
        and 2 * rank % (8 * n_row) == 0
    )
    if not fits:
        return plain_body(covariance, estimate, dual_var, start_basis)
    return fast_body(n_row, n_col, covariance, estimate, dual_var, start_basis)


def solution(mesh):
    return jax.shard_map(
        body,
        mesh=mesh,
        in_specs=(P("row", "col"), P("row", "col"), P("row", "col"), P("row", None)),
        out_specs=(P("row", "col"), P("row", "col")),
        check_vma=False,
    )
```

profile of v0, /device:TPU:0, one launch (start us, length us, event | category | flops | bytes accessed | tf_op | source)
XLA Modules:
  0.0 174.5 jit_solution(11706043899344867150)
XLA Ops:
  0.6 28.7 %shard_map.59.part_ref = f32[8,128,512]{2,1,0:T(8,128)} custom-call(bf16[2048,4096]{1,0:T(8,128)(2,1)} %est_ref.3, bf16[2048,4096]{1,0:T(8,128)(2,1)} %dual_ref.5, bf16[2048,4096]{1,0:T(8,128)(2,1)} %cov_ref.3, f32[2048,128]{1,0:T(8,128)} %basis_ref.1), custom_call_target="tpu_custom_call" | custom-call | tf_op jit(solution)/shard_map/pallas_call | solution.py:168
  29.3 53.5 %shard_map.60 = (f32[8,128,512]{2,1,0:T(8,128)}, f32[4,128,512]{2,1,0:T(8,128)}) custom-call(f32[8,128,512]{2,1,0:T(8,128)} %shard_map.59.part_ref), custom_call_target="tpu_custom_call" | custom-call | tf_op jit(solution)/shard_map/pallas_call | solution.py:354
  82.8 26.1 %shard_map.61 = f32[256,128]{1,0:T(8,128)} custom-call(bf16[2048,4096]{1,0:T(8,128)(2,1)} %est_ref.3, bf16[2048,4096]{1,0:T(8,128)(2,1)} %dual_ref.5, bf16[2048,4096]{1,0:T(8,128)(2,1)} %cov_ref.3, f32[4,128,512]{2,1,0:T(8,128)} %get-tuple-element.4.rows_ref, f32[8,128,512]{2,1,0:T(8,128)} %get-tuple-element.5.cols_ref), custom_call_target="tpu_custom_call" | custom-call | tf_op jit(solution)/shard_map/pallas_call | solution.py:217
  108.9 20.7 %shard_map.62 = f32[8,32,128]{2,1,0:T(8,128)} custom-call(f32[8,32,128]{2,1,0:T(8,128)} %bitcast.2), custom_call_target="tpu_custom_call" | custom-call | tf_op jit(solution)/shard_map/pallas_call | solution.py:437
  129.6 20.4 %shard_map.63.weighted_ref = f32[2048,128]{1,0:T(8,128)} custom-call(f32[256,128]{1,0:T(8,128)} %bitcast.3, f32[4,128,512]{2,1,0:T(8,128)} %get-tuple-element.4.rows_ref), custom_call_target="tpu_custom_call" | custom-call | tf_op jit(solution)/shard_map/pallas_call | solution.py:565
  150.0 24.6 %shard_map.64 = (f32[2048,4096]{1,0:T(8,128)}, bf16[2048,4096]{1,0:T(8,128)(2,1)}) custom-call(f32[2048,128]{1,0:T(8,128)} %shard_map.63.weighted_ref, f32[8,128,512]{2,1,0:T(8,128)} %get-tuple-element.5.cols_ref, bf16[2048,4096]{1,0:T(8,128)(2,1)} %dual_ref.5), custom_call_target="tpu_custom_call" | custom-call | tf_op jit(solution)/shard_map/pallas_call | solution.py:533
where the time goes:
time: 175 us
  Pallas kernels  174 us (99%)
    pallas_call x1, Pallas kernels, spread(): pl.pallas_call(kernel, in_specs=[VMEM], out_specs=(VMEM, VMEM), out_shape...  53.5 us
    pallas_call x1, Pallas kernels, image_parts(): pl.pallas_call(image_kernel, grid=(cols_tile // piece,), in_specs=[pl.Blo...  28.7 us
    pallas_call x1, Pallas kernels, moment_terms(): pl.pallas_call(moment_kernel, grid=(rows_tile // depth,), in_specs=[pl.Bl...  26.1 us
    pallas_call x1, Pallas kernels, finish(): pl.pallas_call(finish_kernel, grid=(rows_tile // depth,), in_specs=[pl.Bl...  24.6 us
    pallas_call x1, Pallas kernels, total(): pl.pallas_call(functools.partial(total_kernel, n_row, n_col), in_specs=[V...  20.7 us
    pallas_call x1, Pallas kernels, fast_body(): pl.pallas_call(weight_kernel, in_specs=[VMEM, VMEM], out_specs=VMEM, out_...  20.4 us

commit v1 on v0

--- a/solution.py
+++ b/solution.py
@@ -121,6 +121,8 @@
 MESH = pl.DeviceIdType.MESH
 VMEM = pl.BlockSpec(memory_space=pltpu.VMEM)
 VMEM_BYTES = 60 * 1024 * 1024
+FULL_VMEM = 67043328
+LOADS_AHEAD = 3
 
 
 def high_dot(left_side, right_side, dims):
@@ -134,110 +136,42 @@
     return upper, (value - upper.astype(jnp.float32)).astype(jnp.bfloat16)
 
 
-def image_kernel(est_ref, dual_ref, cov_ref, basis_ref, out_ref, left_ref, acc_ref):
-    blocks, both, depth = left_ref.shape
-    half = both // 2
-
-    @pl.when(pl.program_id(0) == 0)
-    def _():
-        for index in range(blocks):
-            upper, lower = split(basis_ref[index * depth : (index + 1) * depth, :].T)
-            left_ref[index, :half] = upper
-            left_ref[index, half:] = lower
-
-    acc_ref[...] = jnp.zeros_like(acc_ref)
-
-    def step(block, carry):
-        rows = pl.ds(pl.multiple_of(block * depth, depth), depth)
-        shifted = penalty * (
-            est_ref[rows, :].astype(jnp.float32) - dual_ref[rows, :].astype(jnp.float32)
-        ) - cov_ref[rows, :].astype(jnp.float32)
-        upper, lower = split(shifted)
-        acc_ref[...] += jnp.dot(left_ref[block], upper, preferred_element_type=jnp.float32)
-        acc_ref[:half] += jnp.dot(left_ref[block, :half], lower, preferred_element_type=jnp.float32)
-        return carry
-
-    lax.fori_loop(0, blocks, step, 0)
-    out_ref[0] = acc_ref[:half] + acc_ref[half:]
-
-
-def image_parts(matrices, start_basis, piece):
-    rows_tile, cols_tile = matrices[0].shape
-    rank = start_basis.shape[1]
-    depth = min(256, rows_tile)
-    return pl.pallas_call(
-        image_kernel,
-        grid=(cols_tile // piece,),
-        in_specs=[pl.BlockSpec((rows_tile, piece), lambda step: (0, step))] * 3
-        + [pl.BlockSpec(start_basis.shape, lambda step: (0, 0))],
-        out_specs=pl.BlockSpec((1, rank, piece), lambda step: (step, 0, 0)),
-        out_shape=jax.ShapeDtypeStruct((cols_tile // piece, rank, piece), jnp.float32),
-        scratch_shapes=[
-            pltpu.VMEM((rows_tile // depth, 2 * rank, depth), jnp.bfloat16),
-            pltpu.VMEM((2 * rank, piece), jnp.float32),
-        ],
-        compiler_params=pltpu.CompilerParams(
-            dimension_semantics=("arbitrary",), vmem_limit_bytes=VMEM_BYTES
-        ),
-    )(*matrices, start_basis)
-
-
-def moment_kernel(est_ref, dual_ref, cov_ref, rows_ref, cols_ref, out_ref, right_ref):
-    count, rank, piece = cols_ref.shape
-
-    @pl.when(pl.program_id(0) == 0)
-    def _():
-        for k in range(count):
-            flat = cols_ref[k].T
-            scaled_upper, scaled_lower = split(penalty * flat)
-            upper, lower = split(flat)
-            right_ref[0, k, :, :rank] = scaled_upper
-            right_ref[0, k, :, rank:] = scaled_lower
-            right_ref[1, k, :, :rank] = -scaled_upper
-            right_ref[1, k, :, rank:] = -scaled_lower
-            right_ref[2, k, :, :rank] = -upper
-            right_ref[2, k, :, rank:] = -lower
-        own = cols_ref[lax.axis_index("row")]
-        out_ref[:rank] = high_dot(own, own, ((1,), (1,)))
-        out_ref[rank:] = jnp.zeros((rank, rank), jnp.float32)
-
-    image = jnp.zeros((est_ref.shape[0], 2 * rank), jnp.float32)
-    for k in range(count):
-        where = slice(k * piece, (k + 1) * piece)
-        for which, tile in enumerate((est_ref, dual_ref, cov_ref)):
-            image += jnp.dot(tile[:, where], right_ref[which, k], preferred_element_type=jnp.float32)
-    out_ref[rank:] += high_dot(rows_ref[0], image[:, :rank] + image[:, rank:], ((1,), (0,)))
-
-
-def moment_terms(matrices, rows, cols):
-    rows_tile, cols_tile = matrices[0].shape
-    count, rank, piece = cols.shape
-    depth = min(256, piece)
-    per = piece // depth
-    return pl.pallas_call(
-        moment_kernel,
-        grid=(rows_tile // depth,),
-        in_specs=[pl.BlockSpec((depth, cols_tile), lambda step: (step, 0))] * 3
-        + [
-            pl.BlockSpec((1, rank, depth), lambda step: (step // per, 0, step % per)),
-            pl.BlockSpec(cols.shape, lambda step: (0, 0, 0)),
-        ],
-        out_specs=pl.BlockSpec((2 * rank, rank), lambda step: (0, 0)),
-        out_shape=jax.ShapeDtypeStruct((2 * rank, rank), jnp.float32),
-        scratch_shapes=[pltpu.VMEM((3, count, piece, 2 * rank), jnp.bfloat16)],
-        compiler_params=pltpu.CompilerParams(
-            dimension_semantics=("arbitrary",), vmem_limit_bytes=VMEM_BYTES
-        ),
-    )(*matrices, rows, cols)
-
-
-def spread_kernel(n_row, n_col, part_ref, mc_ref, mr_ref, near, other, zbuf, sems):
+def flip(value, mask, size):
+    result, bit = 0, 1
+    while bit < size:
+        result += (value // bit + mask // bit) % 2 * bit
+        bit *= 2
+    return result
+
+
+def front_kernel(
+    n_row, n_col, est_hbm, dual_hbm, cov_hbm, basis_hbm, mc_ref, mr_ref, out_ref,
+    tiles, basis_ref, left_ref, image_ref, away, near, other, zbuf, load_sems, basis_sem, *sems
+):
+    send1, recv1, send2, recv2, send3, recv3, send4, recv4, send5, recv5, send6, recv6 = sems
     row, col = lax.axis_index("row"), lax.axis_index("col")
+    rank, piece = mc_ref.shape[1:]
+    rows_tile = tiles.shape[2]
     chips = n_row // 2
     chip, core = row // 2, row % 2
     sibling = chip * 2 + 1 - core
     ratio = n_row // n_col
     group = n_row // ratio
+    matrices = (est_hbm, dual_hbm, cov_hbm)
+
+    def load(which, step):
+        there = flip(chip, chips - 1 - step // 2, chips)
+        where = 2 * there + (1 - core + step) % 2
+        columns = pl.ds(pl.multiple_of(where * piece, piece), piece)
+        return pltpu.make_async_copy(
+            matrices[which].at[:, columns], tiles.at[which, where], load_sems.at[which, step]
+        )
+
+    start_basis = pltpu.make_async_copy(basis_hbm, basis_ref, basis_sem)
+    start_basis.start()
+    for step in range(LOADS_AHEAD):
+        for which in range(3):
+            load(which, step).start()
 
     barrier = pltpu.get_barrier_semaphore()
 
@@ -251,129 +185,261 @@
 
     lax.fori_loop(1, n_row, greet_row, 0)
     lax.fori_loop(1, n_col, greet_col, 0)
+
+    start_basis.wait()
+    depth = min(256, rows_tile)
+    for index in range(rows_tile // depth):
+        where = slice(index * depth, (index + 1) * depth)
+        upper, lower = split(basis_ref[where, :].T)
+        left_ref[:rank, where] = upper
+        left_ref[rank:, where] = lower
     pl.semaphore_wait(barrier, n_row - 1 + n_col - 1)
-
-    send1, recv1, send2, recv2, send3, recv3, send4, recv4, send5, recv5, send6, recv6 = sems
 
     def copy(src, dst, send, recv, target):
         return pltpu.make_async_remote_copy(
             src_ref=src, dst_ref=dst, send_sem=send, recv_sem=recv, device_id=target, device_id_type=MESH
         )
 
-    first = []
-    for t in range(chips):
-        there = (chip + 1 + t) % chips
-        first.append(
-            copy(part_ref.at[2 * there + 1 - core], near.at[t], send1.at[t], recv1.at[t], (sibling, col))
-        )
-        first[-1].start()
-    second = []
-    for t in range(chips):
-        there = (chip + 1 + t) % chips
-        first[t].wait_recv()
-        if t < chips - 1:
-            near[t] = near[t] + part_ref[2 * there + core]
-            second.append(
-                copy(near.at[t], other.at[t], send2.at[t], recv2.at[t], (2 * there + core, col))
-            )
-            second[-1].start()
-    total = near[chips - 1] + part_ref[row]
+    def image_part(step):
+        @pl.when(step + LOADS_AHEAD < n_row)
+        def _():
+            for which in range(3):
+                load(which, step + LOADS_AHEAD).start()
+
+        for which in range(3):
+            load(which, step).wait()
+        where = 2 * flip(chip, chips - 1 - step // 2, chips) + (1 - core + step) % 2
+
+        def product(which):
+            return jnp.dot(left_ref[...], tiles[which, where], preferred_element_type=jnp.float32)
+
+        both = penalty * (product(0) - product(1)) - product(2)
+        return both[:rank] + both[rank:]
+
+    def to_sibling(t):
+        return copy(away.at[t], near.at[t], send1.at[t], recv1.at[t], (sibling, col))
+
+    def to_chip(t):
+        there = flip(chip, chips - 1 - t, chips)
+        return copy(near.at[t], other.at[t], send2.at[t], recv2.at[t], (2 * there + core, col))
+
+    def sweep(t, carry):
+        away[t] = image_part(2 * t)
+        to_sibling(t).start()
+        part = image_part(2 * t + 1)
+        to_sibling(t).wait_recv()
+        near[t] = near[t] + part
+
+        @pl.when(t < chips - 1)
+        def _():
+            to_chip(t).start()
+
+        return carry
+
+    lax.fori_loop(0, chips, sweep, 0)
+    total = near[chips - 1]
     for t in range(chips - 1):
-        second[t].wait_recv()
+        to_chip(t).wait_recv()
         total += other[t]
     mc_ref[row] = total
 
     own = mc_ref.at[row]
-    along = []
-    for t in range(n_col - 1):
-        along.append(copy(own, zbuf.at[t], send4.at[t], recv4.at[t], (row, (col + 1 + t) % n_col)))
-        along[-1].start()
-    plane = []
+
+    def along(source, way):
+        block = own if source is None else zbuf.at[source]
+        source = col if source is None else source
+        return copy(
+            block, zbuf.at[source], send4.at[(way + 1) // 2, source], recv4.at[source], (row, col + way)
+        )
+
+    @pl.when(col + 1 < n_col)
+    def _():
+        along(None, 1).start()
+
+    @pl.when(col >= 1)
+    def _():
+        along(None, -1).start()
+
+    def plane(t):
+        return copy(own, own, send3.at[t], recv3.at[t], (2 * flip(chip, t + 1, chips) + core, col))
+
+    def arrived(t):
+        return mc_ref.at[2 * flip(chip, t, chips) + core]
+
+    def pair(t):
+        block = arrived(t)
+        return copy(block, block, send5.at[t], recv5.at[t], (sibling, col))
+
     for t in range(chips - 1):
-        there = (chip + 1 + t) % chips
-        plane.append(copy(own, own, send3.at[t], recv3.at[t], (2 * there + core, col)))
-        plane[-1].start()
-    pair = [copy(own, own, send5.at[0], recv5.at[0], (sibling, col))]
-    pair[0].start()
-
-    slot = row % group
-    onward = []
-    for t in range(n_col - 1):
-        source = (col + n_col - 1 - t) % n_col
+        plane(t).start()
+    pair(0).start()
+
+    def onward(source):
         target = source * ratio + row // group
-        along[t].wait_recv()
-        hop = copy(zbuf.at[t], mr_ref.at[slot], send6.at[t], recv6.at[slot], (target, col))
-
-        @pl.when(target != row)
+        slot = row % group
+        return copy(zbuf.at[source], mr_ref.at[slot], send6.at[source], recv6.at[slot], (target, col)), target
+
+    def serve(source, way):
+        @pl.when((source >= 0) & (source < n_col))
         def _():
-            hop.start()
-
-        @pl.when(target == row)
-        def _():
-            mr_ref[slot] = zbuf[t]
-
-        onward.append((hop, target))
-
-    for t in range(chips - 1):
-        source = 2 * ((chip + chips - 1 - t) % chips) + core
-        arrived = mc_ref.at[source]
-        copy(own, arrived, send3.at[t], recv3.at[t], (row, col)).wait_recv()
-        pair.append(copy(arrived, arrived, send5.at[t + 1], recv5.at[t + 1], (sibling, col)))
-        pair[-1].start()
-    for t in range(chips):
-        source = 2 * ((chip + chips - t) % chips) + 1 - core
-        copy(own, mc_ref.at[source], send5.at[t], recv5.at[t], (sibling, col)).wait_recv()
+            along(source, way).wait_recv()
+
+            @pl.when((col + way >= 0) & (col + way < n_col))
+            def _():
+                along(source, way).start()
+
+            hop, target = onward(source)
+
+            @pl.when(target != row)
+            def _():
+                hop.start()
+
+            @pl.when(target == row)
+            def _():
+                mr_ref[row % group] = zbuf[source]
+
+    def serve_both(s):
+        serve(col - s, 1)
+        serve(col + s, -1)
+
+    image_ref[...] = jnp.zeros_like(image_ref)
+    strip = min(512, rows_tile)
+
+    def apply(where):
+        upper, lower = split(mc_ref[where].T)
+        right = jnp.concatenate([upper, lower], axis=1)
+
+        def one(index, carry):
+            rows = pl.ds(pl.multiple_of(index * strip, strip), strip)
+
+            def product(which):
+                return jnp.dot(tiles[which, where, rows, :], right, preferred_element_type=jnp.float32)
+
+            image_ref[rows, :] += penalty * (product(0) - product(1)) - product(2)
+            return carry
+
+        lax.fori_loop(0, rows_tile // strip, one, 0)
+
+    def apply_chip(t, swap):
+        apply(2 * flip(chip, t, chips) + (core + swap) % 2)
+
+    def wait_pair(t):
+        block = mc_ref.at[2 * flip(chip, t, chips) + 1 - core]
+        copy(own, block, send5.at[t], recv5.at[t], (sibling, col)).wait_recv()
+
+    def take(t):
+        copy(own, arrived(t), send3.at[t - 1], recv3.at[t - 1], (row, col)).wait_recv()
+        pair(t).start()
+
+    apply_chip(0, 0)
+    out_ref[:rank] = high_dot(own[...], own[...], ((1,), (1,)))
+    wait_pair(0)
+    apply_chip(0, 1)
+    served = 1
+    for t in range(1, chips - 1):
+        take(t)
+    serve_both(served)
+    served += 1
+
+    def middle(t, carry):
+        apply_chip(t, 0)
+        wait_pair(t)
+        apply_chip(t, 1)
+        return carry
+
+    lax.fori_loop(1, chips - 1, middle, 0)
+    take(chips - 1)
+    if served < n_col:
+        serve_both(served)
+        served += 1
+    lax.fori_loop(chips - 1, chips, middle, 0)
+    for s in range(served, n_col):
+        serve_both(s)
 
     @pl.when(row // ratio == col)
     def _():
         for k in range(group):
             mr_ref[k] = mc_ref[(row % ratio) * group + k]
 
+    ritz = jnp.zeros((rank, rank), jnp.float32)
     for k in range(group):
         @pl.when((row // ratio != col) & ((row % ratio) * group + k != row))
         def _():
             copy(zbuf.at[0], mr_ref.at[k], send6.at[0], recv6.at[k], (sibling, col)).wait_recv()
 
-    for item in first + second + along + plane + pair:
-        item.wait_send()
-    for hop, target in onward:
-        @pl.when(target != row)
-        def _():
-            hop.wait_send()
-
-
-def spread(parts, n_row, n_col):
-    rank, piece = parts.shape[1:]
+        rows = slice(k * piece, (k + 1) * piece)
+        ritz += high_dot(
+            mr_ref[k], image_ref[rows, :rank] + image_ref[rows, rank:], ((1,), (0,))
+        )
+    out_ref[rank:] = ritz
+
+    for t in range(chips):
+        to_sibling(t).wait_send()
+        pair(t).wait_send()
+    for t in range(chips - 1):
+        to_chip(t).wait_send()
+        plane(t).wait_send()
+
+    @pl.when(col + 1 < n_col)
+    def _():
+        along(None, 1).wait_send()
+
+    @pl.when(col >= 1)
+    def _():
+        along(None, -1).wait_send()
+
+    for s in range(1, n_col):
+        for source, way in ((col - s, 1), (col + s, -1)):
+            @pl.when((source >= 0) & (source < n_col))
+            def _():
+                @pl.when((col + way >= 0) & (col + way < n_col))
+                def _():
+                    along(source, way).wait_send()
+
+                hop, target = onward(source)
+
+                @pl.when(target != row)
+                def _():
+                    hop.wait_send()
+
+
+def front(matrices, start_basis, n_row, n_col):
+    rows_tile, cols_tile = matrices[0].shape
+    rank = start_basis.shape[1]
+    piece = cols_tile // n_row
     chips, ratio = n_row // 2, n_row // n_col
     group = n_row // ratio
     dma = pltpu.SemaphoreType.DMA
-
-    def kernel(part_ref, mc_ref, mr_ref, near, other, zbuf, *sems):
-        spread_kernel(n_row, n_col, part_ref, mc_ref, mr_ref, near, other, zbuf, sems)
-
     return pl.pallas_call(
-        kernel,
-        in_specs=[VMEM],
-        out_specs=(VMEM, VMEM),
+        functools.partial(front_kernel, n_row, n_col),
+        in_specs=[pl.BlockSpec(memory_space=pl.ANY)] * 4,
+        out_specs=(VMEM, VMEM, VMEM),
         out_shape=(
             jax.ShapeDtypeStruct((n_row, rank, piece), jnp.float32),
             jax.ShapeDtypeStruct((group, rank, piece), jnp.float32),
+            jax.ShapeDtypeStruct((2 * rank, rank), jnp.float32),
         ),
         scratch_shapes=[
+            pltpu.VMEM((3, n_row, rows_tile, piece), jnp.bfloat16),
+            pltpu.VMEM((rows_tile, rank), jnp.float32),
+            pltpu.VMEM((2 * rank, rows_tile), jnp.bfloat16),
+            pltpu.VMEM((rows_tile, 2 * rank), jnp.float32),
+            pltpu.VMEM((chips, rank, piece), jnp.float32),
             pltpu.VMEM((chips, rank, piece), jnp.float32),
             pltpu.VMEM((chips - 1, rank, piece), jnp.float32),
-            pltpu.VMEM((n_col - 1, rank, piece), jnp.float32),
+            pltpu.VMEM((n_col, rank, piece), jnp.float32),
+            dma((3, n_row)), dma,
             dma((chips,)), dma((chips,)),
             dma((chips - 1,)), dma((chips - 1,)),
             dma((chips - 1,)), dma((chips - 1,)),
-            dma((n_col - 1,)), dma((n_col - 1,)),
+            dma((2, n_col)), dma((n_col,)),
             dma((chips,)), dma((chips,)),
-            dma((n_col - 1,)), dma((group,)),
+            dma((n_col,)), dma((group,)),
         ],
         compiler_params=pltpu.CompilerParams(
-            collective_id=0, has_side_effects=True, vmem_limit_bytes=VMEM_BYTES
+            collective_id=0, has_side_effects=True, vmem_limit_bytes=FULL_VMEM
         ),
-    )(parts)
+    )(*matrices, start_basis)
 
 
 def total_kernel(n_row, n_col, term_ref, out_ref, terms, part, planes, *sems):
@@ -556,11 +622,8 @@
 def fast_body(n_row, n_col, covariance, estimate, dual_var, start_basis):
     rows_tile, cols_tile = covariance.shape
     rank = start_basis.shape[1]
-    piece = cols_tile // n_row
     matrices = (estimate, dual_var, covariance)
-    parts = image_parts(matrices, start_basis, piece)
-    cols, rows = spread(parts, n_row, n_col)
-    moments = moment_terms(matrices, rows, cols)
+    cols, rows, moments = front(matrices, start_basis, n_row, n_col)
     moments = total(moments, n_row, n_col)
     weighted = pl.pallas_call(
         weight_kernel,
@@ -586,6 +649,9 @@
         and rows_tile % piece == 0
         and rank % 128 == 0
         and 2 * rank % (8 * n_row) == 0
+        and n_row & (n_row - 1) == 0
+        and n_row > LOADS_AHEAD
+        and 6 * rows_tile * cols_tile + 18 * rank * cols_tile <= FULL_VMEM
     )
     if not fits:
         return plain_body(covariance, estimate, dual_var, start_basis)

time: 175 us -> 128 us (0.73)
  Pallas kernels: 174 us -> 127 us
    pallas_call x3 -> x1, Pallas kernels: 108 us -> 64.4 us  [front(): pl.pallas_call(functools.partial(front_kernel, n_row, n_col), in_specs=[p...]
    pallas_call x1, Pallas kernels: 20.7 us -> 17.3 us  [total(): pl.pallas_call(functools.partial(total_kernel, n_row, n_col), in_specs=[V...]
where the time goes in v1:
time: 128 us; the launch traced here: 127 us
  Pallas kernels  127 us (99%)
    pallas_call x1, Pallas kernels, front(): pl.pallas_call(functools.partial(front_kernel, n_row, n_col), in_specs=[p...  64.4 us
    pallas_call x1, Pallas kernels, finish(): pl.pallas_call(finish_kernel, grid=(rows_tile // depth,), in_specs=[pl.Bl...  24.6 us
    pallas_call x1, Pallas kernels, fast_body(): pl.pallas_call(weight_kernel, in_specs=[VMEM, VMEM], out_specs=VMEM, out_...  20.4 us
    pallas_call x1, Pallas kernels, total(): pl.pallas_call(functools.partial(total_kernel, n_row, n_col), in_specs=[V...  17.3 us

profile of v1, /device:TPU:0, one launch (start us, length us, event | category | flops | bytes accessed | tf_op | source)
XLA Modules:
  0.0 127.4 jit_solution(11368816736853766905)
XLA Ops:
  0.6 64.4 %shard_map.59 = (f32[8,128,512]{2,1,0:T(8,128)}, f32[4,128,512]{2,1,0:T(8,128)}, f32[256,128]{1,0:T(8,128)}) custom-call(bf16[2048,4096]{1,0:T(8,128)(2,1)} %est_hbm.1, bf16[2048,4096]{1,0:T(8,128)(2,1)} %dual_ref.1, bf16[2048,4096]{1,0:T(8,128)(2,1)} %cov_hbm.1, f32[2048,128]{1,0:T(8,128)} %basis_hbm.1), custom_call_target="tpu_custom_call" | custom-call | tf_op jit(solution)/shard_map/pallas_call | solution.py:413
  65.1 17.3 %shard_map.60 = f32[8,32,128]{2,1,0:T(8,128)} custom-call(f32[8,32,128]{2,1,0:T(8,128)} %bitcast.3), custom_call_target="tpu_custom_call" | custom-call | tf_op jit(solution)/shard_map/pallas_call | solution.py:503
  82.4 20.4 %shard_map.61.weighted_ref = f32[2048,128]{1,0:T(8,128)} custom-call(f32[256,128]{1,0:T(8,128)} %bitcast.2, f32[4,128,512]{2,1,0:T(8,128)} %get-tuple-element.6.rows_ref), custom_call_target="tpu_custom_call" | custom-call | tf_op jit(solution)/shard_map/pallas_call | solution.py:628
  102.8 24.6 %shard_map.62 = (f32[2048,4096]{1,0:T(8,128)}, bf16[2048,4096]{1,0:T(8,128)(2,1)}) custom-call(f32[2048,128]{1,0:T(8,128)} %shard_map.61.weighted_ref, f32[8,128,512]{2,1,0:T(8,128)} %get-tuple-element.7.cols_ref, bf16[2048,4096]{1,0:T(8,128)(2,1)} %dual_ref.1), custom_call_target="tpu_custom_call" | custom-call | tf_op jit(solution)/shard_map/pallas_call | solution.py:599

commit v2 on v1

v2 whole, which is shorter than its diff:
```python
import functools

import jax
import jax.numpy as jnp
from jax import lax
from jax.experimental import pallas as pl
from jax.experimental.pallas import tpu as pltpu
from jax.sharding import PartitionSpec as P

NS_ITERS = 12


penalty = 0.01
threshold = 0.2
base_level = 10.0
highest = lax.Precision.HIGHEST


def from_root(value, axis, source):
    kept = jnp.where(lax.axis_index(axis) == source, value, 0).astype(value.dtype)
    return lax.psum(kept, axis)


def inner_product(left_side, right_side):
    return lax.dot_general(
        left_side,
        right_side,
        (((0,), (0,)), ((), ())),
        precision=highest,
        preferred_element_type=jnp.float32,
    )


def normalize(mapped, gram_matrix):
    lower_factor = jnp.linalg.cholesky(gram_matrix)
    identity = jnp.eye(gram_matrix.shape[0], dtype=jnp.float32)
    inverse = lax.linalg.triangular_solve(lower_factor, identity, left_side=True, lower=True)
    return jnp.dot(mapped, inverse.T, precision=highest, preferred_element_type=jnp.float32)


def response_of(ritz_matrix):
    identity = jnp.eye(ritz_matrix.shape[0], dtype=jnp.float32)
    square = (
        jnp.dot(ritz_matrix, ritz_matrix, precision=highest, preferred_element_type=jnp.float32)
        + 4.0 * penalty * identity
    )
    frobenius = jnp.sqrt(jnp.sum(square * square))

    def newton(sweep_index, state_pair):
        iterate, partner = state_pair
        factor = 0.5 * (
            3.0 * identity
            - jnp.dot(partner, iterate, precision=highest, preferred_element_type=jnp.float32)
        )
        return (
            jnp.dot(iterate, factor, precision=highest, preferred_element_type=jnp.float32),
            jnp.dot(factor, partner, precision=highest, preferred_element_type=jnp.float32),
        )

    iterate, partner = lax.fori_loop(0, NS_ITERS, newton, (square / frobenius, identity))
    square_root = jnp.sqrt(frobenius) * iterate
    return (ritz_matrix + square_root) / (2.0 * penalty) - base_level * identity


def column_basis(shifted, row_basis):
    partial_terms = lax.dot_general(
        shifted,
        row_basis,
        (((0,), (0,)), ((), ())),
        precision=highest,
        preferred_element_type=jnp.float32,
    )
    mapped = lax.psum(partial_terms, "row")
    gram_matrix = lax.psum(inner_product(mapped, mapped), "col")
    return normalize(mapped, gram_matrix)


def row_image(shifted, col_basis):
    local_terms = jnp.dot(shifted, col_basis, precision=highest, preferred_element_type=jnp.float32)
    return lax.psum(local_terms, "col")


def row_inner(left_side, right_side):
    return lax.psum(inner_product(left_side, right_side), "row")


def plain_body(covariance, estimate, dual_var, start_basis):
    shifted = penalty * (
        estimate.astype(jnp.float32) - dual_var.astype(jnp.float32)
    ) - covariance.astype(jnp.float32)
    rows_tile = shifted.shape[0]
    cols_tile = shifted.shape[1]
    row_basis = start_basis
    col_basis = column_basis(shifted, row_basis)
    blocks_per_column = lax.axis_size("row") // lax.axis_size("col")
    row_index = lax.axis_index("row")
    own_block = lax.dynamic_slice_in_dim(
        col_basis, row_index % blocks_per_column * rows_tile, rows_tile, 0
    )
    row_basis = from_root(own_block, "col", row_index // blocks_per_column)
    product = row_image(shifted, col_basis)
    raw_ritz = row_inner(row_basis, product)
    ritz_matrix = 0.5 * (raw_ritz + raw_ritz.T)
    response = response_of(ritz_matrix)
    weighted = jnp.dot(row_basis, response, precision=highest, preferred_element_type=jnp.float32)
    theta_tile = lax.dot_general(
        weighted,
        col_basis,
        (((1,), (1,)), ((), ())),
        precision=highest,
        preferred_element_type=jnp.float32,
    )
    row_ids = row_index * rows_tile + lax.broadcasted_iota(jnp.int32, (rows_tile, 1), 0)
    col_ids = lax.axis_index("col") * cols_tile + lax.broadcasted_iota(jnp.int32, (1, cols_tile), 1)
    theta_tile = theta_tile + jnp.where(row_ids == col_ids, base_level, 0.0)
    mixture = theta_tile + dual_var.astype(jnp.float32)
    clipped = jnp.clip(mixture, -threshold, threshold)
    return (mixture - clipped, clipped.astype(jnp.bfloat16))


MESH = pl.DeviceIdType.MESH
VMEM = pl.BlockSpec(memory_space=pltpu.VMEM)
VMEM_BYTES = 60 * 1024 * 1024
FULL_VMEM = 67043328
LOADS_AHEAD = 3
CHUNKS = 4
FINISH_ROWS = 512


def high_dot(left_side, right_side, dims):
    return lax.dot_general(
        left_side, right_side, (dims, ((), ())), precision=highest, preferred_element_type=jnp.float32
    )


def split(value):
    upper = value.astype(jnp.bfloat16)
    return upper, (value - upper.astype(jnp.float32)).astype(jnp.bfloat16)


def remote(src, dst, send, recv, target):
    return pltpu.make_async_remote_copy(
        src_ref=src, dst_ref=dst, send_sem=send, recv_sem=recv, device_id=target, device_id_type=MESH
    )


def flip(value, mask, size):
    result, bit = 0, 1
    while bit < size:
        result += (value // bit + mask // bit) % 2 * bit
        bit *= 2
    return result


def front_kernel(
    n_row, n_col, est_hbm, dual_hbm, cov_hbm, basis_hbm, weights_hbm, right_hbm, low_hbm,
    tiles, basis_ref, left_ref, image_ref, away, near, other, zbuf, mc_ref, mr_ref,
    gram, gram_terms, gram_part, gram_planes, gram_sum,
    inner, inner_terms, inner_part, inner_planes, inner_sum,
    inverse_ref, ritz_ref, iterate_ref, partner_ref,
    load_sems, basis_sem, store_sems, *sems
):
    send1, recv1, send2, recv2, send3, recv3, send4, recv4, send5, recv5, send6, recv6 = sems[:12]
    gram_scatter, gram_across, gram_gather, gram_finish, gram_drain = sum_over_mesh(
        n_row, n_col, gram, gram_terms, gram_part, gram_planes, gram_sum, sems[12:18]
    )
    inner_scatter, inner_across, inner_gather, inner_finish, inner_drain = sum_over_mesh(
        n_row, n_col, inner, inner_terms, inner_part, inner_planes, inner_sum, sems[18:24]
    )
    copy = remote
    row, col = lax.axis_index("row"), lax.axis_index("col")
    rank, piece = mc_ref.shape[1:]
    rows_tile = tiles.shape[2]
    chips = n_row // 2
    chip, core = row // 2, row % 2
    sibling = chip * 2 + 1 - core
    ratio = n_row // n_col
    group = n_row // ratio
    cut = rank // CHUNKS
    home = row // ratio

    def works(left, right):
        odd = (left + right) % 2
        return (left == right) | ((odd == 1) & (left < right)) | ((odd == 0) & (left > right))

    working = works(home, col)
    matrices = (est_hbm, dual_hbm, cov_hbm)

    def load(which, step):
        there = flip(chip, chips - 1 - step // 2, chips)
        where = 2 * there + (1 - core + step) % 2
        columns = pl.ds(pl.multiple_of(where * piece, piece), piece)
        return pltpu.make_async_copy(
            matrices[which].at[:, columns], tiles.at[which, where], load_sems.at[which, step]
        )

    start_basis = pltpu.make_async_copy(basis_hbm, basis_ref, basis_sem)
    start_basis.start()
    for step in range(LOADS_AHEAD):
        for which in range(3):
            load(which, step).start()

    barrier = pltpu.get_barrier_semaphore()

    def greet_row(t, carry):
        pl.semaphore_signal(barrier, inc=1, device_id=((row + t) % n_row, col), device_id_type=MESH)
        return carry

    def greet_col(t, carry):
        pl.semaphore_signal(barrier, inc=1, device_id=(row, (col + t) % n_col), device_id_type=MESH)
        return carry

    lax.fori_loop(1, n_row, greet_row, 0)
    lax.fori_loop(1, n_col, greet_col, 0)

    start_basis.wait()
    depth = min(256, rows_tile)
    for index in range(rows_tile // depth):
        where = slice(index * depth, (index + 1) * depth)
        upper, lower = split(basis_ref[where, :].T)
        left_ref[:rank, where] = upper
        left_ref[rank:, where] = lower
    pl.semaphore_wait(barrier, n_row - 1 + n_col - 1)

    def image_part(step):
        @pl.when(step + LOADS_AHEAD < n_row)
        def _():
            for which in range(3):
                load(which, step + LOADS_AHEAD).start()

        for which in range(3):
            load(which, step).wait()
        where = 2 * flip(chip, chips - 1 - step // 2, chips) + (1 - core + step) % 2

        def product(which):
            return jnp.dot(left_ref[...], tiles[which, where], preferred_element_type=jnp.float32)

        both = penalty * (product(0) - product(1)) - product(2)
        return both[:rank] + both[rank:]

    def to_sibling(t):
        return copy(away.at[t], near.at[t], send1.at[t], recv1.at[t], (sibling, col))

    def to_chip(t):
        there = flip(chip, chips - 1 - t, chips)
        return copy(near.at[t], other.at[t], send2.at[t], recv2.at[t], (2 * there + core, col))

    def sweep(t, carry):
        away[t] = image_part(2 * t)
        to_sibling(t).start()
        part = image_part(2 * t + 1)
        to_sibling(t).wait_recv()
        near[t] = near[t] + part

        @pl.when(t < chips - 1)
        def _():
            to_chip(t).start()

        return carry

    lax.fori_loop(0, chips, sweep, 0)
    total = near[chips - 1]
    for t in range(chips - 1):
        to_chip(t).wait_recv()
        total += other[t]
    mc_ref[row] = total

    own = mc_ref.at[row]

    def along(source, way, part):
        block = own if source is None else zbuf.at[source]
        source = col if source is None else source
        lines = pl.ds(part * cut, cut)
        return copy(
            block.at[lines], zbuf.at[source, lines],
            send4.at[(way + 1) // 2, source, part], recv4.at[source, part], (row, col + way),
        )

    def start_along(parts):
        for part in parts:
            @pl.when(col + 1 < n_col)
            def _():
                along(None, 1, part).start()

            @pl.when(col >= 1)
            def _():
                along(None, -1, part).start()

    wide = double(own[...], 0)
    wide = lax.dot_general(
        wide, wide, (((1,), (1,)), ((), ())), preferred_element_type=jnp.float32
    )
    wide = wide[:rank] + wide[rank:]
    gram[...] = (wide[:, :rank] + wide[:, rank:]).reshape(gram.shape)
    gram_scatter()
    start_along(range(CHUNKS // 2))

    def plane(t):
        return copy(own, own, send3.at[t], recv3.at[t], (2 * flip(chip, t + 1, chips) + core, col))

    def arrived(t):
        return mc_ref.at[2 * flip(chip, t, chips) + core]

    def pair(t):
        block = arrived(t)
        return copy(block, block, send5.at[t], recv5.at[t], (sibling, col))

    for t in range(chips - 2):
        plane(t).start()
    pair(0).start()

    def onward(source, part):
        target = source * ratio + row // group
        slot = row % group
        lines = pl.ds(part * cut, cut)
        hop = copy(
            zbuf.at[source, lines], mr_ref.at[slot, lines],
            send6.at[source, part], recv6.at[slot, part], (target, col),
        )
        return hop, target

    def send_onward(source, part):
        hop, target = onward(source, part)

        @pl.when(target != row)
        def _():
            hop.start()

        @pl.when(target == row)
        def _():
            lines = slice(part * cut, (part + 1) * cut)
            mr_ref[row % group, lines] = zbuf[source, lines]

    def serve(source, way, part):
        @pl.when((source >= 0) & (source < n_col))
        def _():
            along(source, way, part).wait_recv()

            @pl.when((col + way >= 0) & (col + way < n_col))
            def _():
                along(source, way, part).start()

            @pl.when(works(source, col))
            def _():
                send_onward(source, part)

    def serve_half(hop, half):
        for part in range(CHUNKS // 2):
            for k in range(2):
                @pl.when(half == k)
                def _():
                    serve(col - hop, 1, k * (CHUNKS // 2) + part)
                    serve(col + hop, -1, k * (CHUNKS // 2) + part)

    image_ref[...] = jnp.zeros_like(image_ref)
    strip = min(512, rows_tile)

    def apply(where):
        upper, lower = split(mc_ref[where].T)
        right = jnp.concatenate([upper, lower], axis=1)

        def one(index, carry):
            rows = pl.ds(pl.multiple_of(index * strip, strip), strip)

            def product(which):
                return jnp.dot(tiles[which, where, rows, :], right, preferred_element_type=jnp.float32)

            image_ref[rows, :] += penalty * (product(0) - product(1)) - product(2)
            return carry

        lax.fori_loop(0, rows_tile // strip, one, 0)

    def apply_chip(t, swap):
        apply(2 * flip(chip, t, chips) + (core + swap) % 2)

    def wait_pair(t):
        block = mc_ref.at[2 * flip(chip, t, chips) + 1 - core]
        copy(own, block, send5.at[t], recv5.at[t], (sibling, col)).wait_recv()

    def take(t):
        copy(own, arrived(t), send3.at[t - 1], recv3.at[t - 1], (row, col)).wait_recv()
        pair(t).start()

    def stage(j, carry):
        t = j // 2

        @pl.when(j == 2)
        def _():
            gram_gather()
            plane(chips - 2).start()
            for other_chip in range(1, chips - 1):
                take(other_chip)

        @pl.when(j == n_row - 3)
        def _():
            take(chips - 1)

        @pl.when(j % 2 == 1)
        def _():
            wait_pair(t)

        @pl.when(working)
        def _():
            apply_chip(t, j % 2)

        @pl.when(j == 0)
        def _():
            gram_across()
            start_along(range(CHUNKS // 2, CHUNKS))

        @pl.when(t + 1 < n_col)
        def _():
            serve_half(t + 1, j % 2)

        @pl.when(j == 2 * n_col - 3)
        def _():
            for source in range(n_col):
                @pl.when((source != col) & jnp.logical_not(works(source, col)))
                def _():
                    for part in range(CHUNKS):
                        send_onward(source, part)

        return carry

    lax.fori_loop(0, n_row, stage, 0)
    gram_finish()
    third = -(-rank // 24) * 8
    inverse_ref[...] = gram_sum[...].reshape(rank, rank)

    def wait_rows():
        for k in range(group):
            @pl.when((home != col) & ((row % ratio) * group + k != row))
            def _():
                for part in range(CHUNKS):
                    lines = pl.ds(part * cut, cut)
                    copy(
                        zbuf.at[0, lines], mr_ref.at[k, lines],
                        send6.at[0, part], recv6.at[k, part], (sibling, col),
                    ).wait_recv()

    @pl.when(home == col)
    def _():
        for k in range(group):
            mr_ref[k] = mc_ref[(row % ratio) * group + k]

    @pl.when(working)
    def _():
        wait_rows()
        ritz = jnp.zeros((2 * rank, 2 * rank), jnp.float32)
        for k in range(group):
            rows = slice(k * piece, (k + 1) * piece)
            ritz += jnp.dot(
                double(mr_ref[k], 0),
                double(image_ref[rows, :rank] + image_ref[rows, rank:], 1),
                preferred_element_type=jnp.float32,
            )
        ritz = ritz[:rank] + ritz[rank:]
        times = jnp.where(home == col, 1.0, 2.0)
        inner[...] = (times * (ritz[:, :rank] + ritz[:, rank:])).reshape(inner.shape)

    @pl.when(jnp.logical_not(working))
    def _():
        inner[...] = jnp.zeros_like(inner)

    inner_scatter()
    inverse_ref[...] = invert(inverse_ref[...], 0, third)
    inner_across()
    inverse_ref[...] = invert(inverse_ref[...], third, 2 * third)
    inner_gather()
    inverse_ref[...] = invert(inverse_ref[...], 2 * third, rank)

    def prepare(k, carry):
        upper, lower = split(mc_ref[k])
        tiles[0, k, :rank, :] = upper
        tiles[0, k, rank : 2 * rank, :] = upper
        tiles[1, k, :rank, :] = lower
        return carry

    lax.fori_loop(0, n_row, prepare, 0)
    store_right = pltpu.make_async_copy(
        tiles.at[0, :, pl.ds(0, 2 * rank)], right_hbm, store_sems.at[0]
    )
    store_low = pltpu.make_async_copy(tiles.at[1, :, pl.ds(0, rank)], low_hbm, store_sems.at[1])
    store_right.start()
    store_low.start()
    inner_finish()
    update = response_times_inverse(
        inner_sum[...].reshape(rank, rank), inverse_ref, ritz_ref, iterate_ref, partner_ref
    )
    partner_ref[...] = update

    @pl.when(jnp.logical_not(working))
    def _():
        wait_rows()

    for k in range(group):
        tiles[2, 0, k * piece : (k + 1) * piece, : 2 * rank] = double(
            fine_dot(mr_ref[k].T, partner_ref[...]), 1
        )
    store_weights = pltpu.make_async_copy(
        tiles.at[2, 0, :, pl.ds(0, 2 * rank)], weights_hbm, store_sems.at[2]
    )
    store_weights.start()
    gram_drain()
    inner_drain()
    for t in range(chips):
        to_sibling(t).wait_send()
        pair(t).wait_send()
    for t in range(chips - 1):
        to_chip(t).wait_send()
        plane(t).wait_send()

    for part in range(CHUNKS):
        @pl.when(col + 1 < n_col)
        def _():
            along(None, 1, part).wait_send()

        @pl.when(col >= 1)
        def _():
            along(None, -1, part).wait_send()

        for s in range(1, n_col):
            for source, way in ((col - s, 1), (col + s, -1)):
                @pl.when((source >= 0) & (source < n_col))
                def _():
                    @pl.when((col + way >= 0) & (col + way < n_col))
                    def _():
                        along(source, way, part).wait_send()

                    hop, target = onward(source, part)

                    @pl.when(target != row)
                    def _():
                        hop.wait_send()

    store_right.wait()
    store_low.wait()
    store_weights.wait()


def front(matrices, start_basis, n_row, n_col):
    rows_tile, cols_tile = matrices[0].shape
    rank = start_basis.shape[1]
    piece = cols_tile // n_row
    chips, ratio = n_row // 2, n_row // n_col
    group = n_row // ratio
    dma = pltpu.SemaphoreType.DMA
    block = (rank // n_row, rank)
    sum_buffers = [
        pltpu.VMEM((n_row, *block), jnp.float32),
        pltpu.VMEM((n_row, *block), jnp.float32),
        pltpu.VMEM(block, jnp.float32),
        pltpu.VMEM((n_col, *block), jnp.float32),
        pltpu.VMEM((n_row, *block), jnp.float32),
    ]
    sum_sems = [dma((n_row,))] * 2 + [dma((n_col,))] * 2 + [dma((n_row,))] * 2
    return pl.pallas_call(
        functools.partial(front_kernel, n_row, n_col),
        in_specs=[pl.BlockSpec(memory_space=pl.ANY)] * 4,
        out_specs=[pl.BlockSpec(memory_space=pl.ANY)] * 3,
        out_shape=(
            jax.ShapeDtypeStruct((rows_tile, 2 * rank), jnp.bfloat16),
            jax.ShapeDtypeStruct((n_row, 2 * rank, piece), jnp.bfloat16),
            jax.ShapeDtypeStruct((n_row, rank, piece), jnp.bfloat16),
        ),
        scratch_shapes=[
            pltpu.VMEM((3, n_row, rows_tile, piece), jnp.bfloat16),
            pltpu.VMEM((rows_tile, rank), jnp.float32),
            pltpu.VMEM((2 * rank, rows_tile), jnp.bfloat16),
            pltpu.VMEM((rows_tile, 2 * rank), jnp.float32),
            pltpu.VMEM((chips, rank, piece), jnp.float32),
            pltpu.VMEM((chips, rank, piece), jnp.float32),
            pltpu.VMEM((chips - 1, rank, piece), jnp.float32),
            pltpu.VMEM((n_col, rank, piece), jnp.float32),
            pltpu.VMEM((n_row, rank, piece), jnp.float32),
            pltpu.VMEM((group, rank, piece), jnp.float32),
            *sum_buffers, *sum_buffers,
            *[pltpu.VMEM((rank, rank), jnp.float32)] * 4,
            dma((3, n_row)), dma, dma((3,)),
            dma((chips,)), dma((chips,)),
            dma((chips - 1,)), dma((chips - 1,)),
            dma((chips - 1,)), dma((chips - 1,)),
            dma((2, n_col, CHUNKS)), dma((n_col, CHUNKS)),
            dma((chips,)), dma((chips,)),
            dma((n_col, CHUNKS)), dma((group, CHUNKS)),
            *sum_sems, *sum_sems,
        ],
        compiler_params=pltpu.CompilerParams(
            collective_id=0, has_side_effects=True, vmem_limit_bytes=FULL_VMEM
        ),
    )(*matrices, start_basis)


def sum_over_mesh(n_row, n_col, term, terms, part, planes, out, sems):
    send1, recv1, send2, recv2, send3, recv3 = sems
    row, col = lax.axis_index("row"), lax.axis_index("col")

    def first(t):
        there = (row + t) % n_row
        return remote(term.at[there], terms.at[t], send1.at[t], recv1.at[t], (there, col))

    def second(t):
        there = (col + t) % n_col
        return remote(part, planes.at[col], send2.at[t], recv2.at[col], (row, there))

    def third(t):
        there = (row + t) % n_row
        return remote(out.at[row], out.at[row], send3.at[t], recv3.at[t], (there, col))

    def scatter():
        for t in range(1, n_row):
            first(t).start()

    def across():
        summed = term[row]
        for t in range(1, n_row):
            first(t).wait_recv()
            summed += terms[t]
        part[...] = summed
        for t in range(1, n_col):
            second(t).start()
        planes[col] = summed

    def gather():
        for t in range(1, n_col):
            source = (col + t) % n_col
            remote(part, planes.at[source], send2.at[t], recv2.at[source], (row, source)).wait_recv()
        out[row] = jnp.sum(planes[...], axis=0)
        for t in range(1, n_row):
            third(t).start()

    def finish():
        for t in range(1, n_row):
            source = (row + n_row - t) % n_row
            remote(out.at[row], out.at[source], send3.at[t], recv3.at[t], (source, col)).wait_recv()

    def drain():
        for t in range(1, n_row):
            first(t).wait_send()
            third(t).wait_send()
        for t in range(1, n_col):
            second(t).wait_send()

    return scatter, across, gather, finish, drain


def invert(value, first, last):
    rank = value.shape[0]
    row_ids = lax.broadcasted_iota(jnp.int32, (rank, rank), 0)
    col_ids = lax.broadcasted_iota(jnp.int32, (rank, rank), 1)
    line_ids = lax.broadcasted_iota(jnp.int32, (1, rank), 1)
    for k in range(first, last):
        pivot = 1.0 / value[k : k + 1, k : k + 1]
        column = value[:, k : k + 1]
        line = jnp.where(line_ids == k, 1.0, value[k : k + 1, :]) * pivot
        value = jnp.where(
            row_ids == k, line, jnp.where(col_ids == k, 0.0, value) - column * line
        )
    return value


def double(value, axis):
    return jnp.concatenate(split(value), axis=axis)


def fine_dot(left_side, right_side):
    right = double(right_side, 1)
    both = jnp.dot(
        double(left_side, 1),
        jnp.concatenate([right, right], axis=0),
        preferred_element_type=jnp.float32,
    )
    width = right_side.shape[1]
    return both[:, :width] + both[:, width:]


def response_times_inverse(raw, inverse_ref, ritz_ref, iterate_ref, partner_ref):
    rank = raw.shape[0]
    row_ids = lax.broadcasted_iota(jnp.int32, (rank, rank), 0)
    col_ids = lax.broadcasted_iota(jnp.int32, (rank, rank), 1)
    identity = jnp.where(row_ids == col_ids, 1.0, 0.0)
    ritz_ref[...] = fine_dot(inverse_ref[...], 0.5 * (raw + raw.T))
    square = fine_dot(ritz_ref[...], ritz_ref[...]) + 4.0 * penalty * identity
    frobenius = jnp.sqrt(jnp.sum(square * square.T, keepdims=True))
    start = square / frobenius
    factor = 1.5 * identity - 0.5 * start
    iterate_ref[...] = fine_dot(start, factor)
    partner_ref[...] = factor

    def newton(step, carry):
        iterate, partner = iterate_ref[...], partner_ref[...]
        factor = 1.5 * identity - 0.5 * fine_dot(partner, iterate)
        iterate_ref[...] = fine_dot(iterate, factor)
        partner_ref[...] = fine_dot(factor, partner)
        return carry

    lax.fori_loop(1, NS_ITERS, newton, 0)
    root = jnp.sqrt(frobenius) * iterate_ref[...]
    response = (ritz_ref[...] + root) / (2.0 * penalty) - base_level * identity
    return fine_dot(response, inverse_ref[...])


def finish_kernel(weights_ref, right_ref, low_ref, dual_ref, est_ref, clip_ref):
    step = pl.program_id(0)
    count, rank, piece = low_ref.shape
    depth = dual_ref.shape[0]
    n_grid = pl.num_programs(0)
    row_start = (lax.axis_index("row") * n_grid + step) * depth
    gap = (
        lax.broadcasted_iota(jnp.int32, (depth, piece), 1)
        - lax.broadcasted_iota(jnp.int32, (depth, piece), 0)
    )
    for k in range(count):
        where = slice(k * piece, (k + 1) * piece)
        col_start = lax.axis_index("col") * (count * piece) + k * piece
        theta = jnp.dot(weights_ref[...], right_ref[k], preferred_element_type=jnp.float32)
        theta += jnp.dot(weights_ref[:, :rank], low_ref[k], preferred_element_type=jnp.float32)
        theta += jnp.where(gap == row_start - col_start, base_level, 0.0)
        mixture = theta + dual_ref[:, where].astype(jnp.float32)
        clipped = jnp.clip(mixture, -threshold, threshold)
        est_ref[:, where] = mixture - clipped
        clip_ref[:, where] = clipped.astype(jnp.bfloat16)


def finish(weights, right, low, dual_var):
    rows_tile, cols_tile = dual_var.shape
    depth = min(FINISH_ROWS, rows_tile)
    wide = pl.BlockSpec((depth, cols_tile), lambda step: (step, 0))
    return pl.pallas_call(
        finish_kernel,
        grid=(rows_tile // depth,),
        in_specs=[
            pl.BlockSpec((depth, weights.shape[1]), lambda step: (step, 0)),
            pl.BlockSpec(right.shape, lambda step: (0, 0, 0)),
            pl.BlockSpec(low.shape, lambda step: (0, 0, 0)),
            wide,
        ],
        out_specs=(wide, wide),
        out_shape=(
            jax.ShapeDtypeStruct(dual_var.shape, jnp.float32),
            jax.ShapeDtypeStruct(dual_var.shape, jnp.bfloat16),
        ),
        compiler_params=pltpu.CompilerParams(
            dimension_semantics=("arbitrary",), vmem_limit_bytes=VMEM_BYTES
        ),
    )(weights, right, low, dual_var)


def fast_body(n_row, n_col, covariance, estimate, dual_var, start_basis):
    rows_tile, cols_tile = covariance.shape
    rank = start_basis.shape[1]
    matrices = (estimate, dual_var, covariance)
    weights, right, low = front(matrices, start_basis, n_row, n_col)
    return finish(weights, right, low, dual_var)


def body(covariance, estimate, dual_var, start_basis):
    n_row, n_col = lax.axis_size("row"), lax.axis_size("col")
    rows_tile, cols_tile = covariance.shape
    rank = start_basis.shape[1]
    piece = cols_tile // n_row
    fits = (
        n_row % 2 == 0
        and n_row % n_col == 0
        and cols_tile % n_row == 0
        and piece % 128 == 0
        and rows_tile % piece == 0
        and rank % 128 == 0
        and rank % (8 * n_row) == 0
        and 2 * rank <= min(rows_tile, piece)
        and n_row & (n_row - 1) == 0
        and n_row >= max(8, 2 * n_col)
        and rank % (8 * CHUNKS) == 0
        and n_row > LOADS_AHEAD
        and 6 * rows_tile * cols_tile + 19 * rank * cols_tile <= FULL_VMEM
    )
    if not fits:
        return plain_body(covariance, estimate, dual_var, start_basis)
    return fast_body(n_row, n_col, covariance, estimate, dual_var, start_basis)


def solution(mesh):
    return jax.shard_map(
        body,
        mesh=mesh,
        in_specs=(P("row", "col"), P("row", "col"), P("row", "col"), P("row", None)),
        out_specs=(P("row", "col"), P("row", "col")),
        check_vma=False,
    )
```

time: 128 us -> 110 us (0.86)
  Pallas kernels: 127 us -> 109 us
    pallas_call x2 -> x0, Pallas kernels: 37.7 us -> none  [the longest x1 20.4 us: fast_body(): pl.pallas_call(weight_kernel, in_specs=[VMEM, VMEM], out_specs=VMEM, out_...]
    pallas_call x1, Pallas kernels: 64.4 us -> 84.5 us  [front(): pl.pallas_call(functools.partial(front_kernel, n_row, n_col), in_specs=[p...]
where the time goes in v2:
time: 110 us
  Pallas kernels  109 us (99%)
    pallas_call x1, Pallas kernels, front(): pl.pallas_call(functools.partial(front_kernel, n_row, n_col), in_specs=[p...  84.5 us
    pallas_call x1, Pallas kernels, finish(): pl.pallas_call(finish_kernel, grid=(rows_tile // depth,), in_specs=[pl.Bl...  24.6 us

profile of v2, /device:TPU:0, one launch (start us, length us, event | category | flops | bytes accessed | tf_op | source)
XLA Modules:
  0.0 109.7 jit_solution(3390877186696413792)
XLA Ops:
  0.6 84.5 %shard_map.59 = (bf16[2048,256]{1,0:T(8,128)(2,1)}, bf16[8,256,512]{2,1,0:T(8,128)(2,1)}, bf16[8,128,512]{2,1,0:T(8,128)(2,1)}) custom-call(bf16[2048,4096]{1,0:T(8,128)(2,1)} %est_hbm.1, bf16[2048,4096]{1,0:T(8,128)(2,1)} %dual_ref.1, bf16[2048,4096]{1,0:T(8,128)(2,1)} %cov_hbm.1, f32[2048,128]{1,0:T(8,128)} %basis_hbm.1), custom_call_target="tpu_custom_call" | custom-call | tf_op jit(solution)/shard_map/pallas_call | solution.py:557
  85.1 24.6 %shard_map.60 = (f32[2048,4096]{1,0:T(8,128)}, bf16[2048,4096]{1,0:T(8,128)(2,1)}) custom-call(bf16[2048,256]{1,0:T(8,128)(2,1)} %get-tuple-element.5.weights_ref, bf16[8,256,512]{2,1,0:T(8,128)(2,1)} %get-tuple-element.6.right_ref, bf16[8,128,512]{2,1,0:T(8,128)(2,1)} %get-tuple-element.7.low_ref, bf16[2048,4096]{1,0:T(8,128)(2,1)} %dual_ref.1), custom_call_target="tpu_custom_call" | custom-call | tf_op jit(solution)/shard_map/pallas_call | solution.py:729

commit v3 on v2

--- a/solution.py
+++ b/solution.py
@@ -120,11 +120,12 @@
 
 MESH = pl.DeviceIdType.MESH
 VMEM = pl.BlockSpec(memory_space=pltpu.VMEM)
-VMEM_BYTES = 60 * 1024 * 1024
+VMEM_BYTES = 40 * 1024 * 1024
 FULL_VMEM = 67043328
-LOADS_AHEAD = 3
+FRONT_VMEM = 46 * 1024 * 1024 + 512 * 1024
+LOADS_AHEAD = 2
 CHUNKS = 4
-FINISH_ROWS = 512
+FINISH_ROWS = 256
 
 
 def high_dot(left_side, right_side, dims):
@@ -153,8 +154,8 @@
 
 
 def front_kernel(
-    n_row, n_col, est_hbm, dual_hbm, cov_hbm, basis_hbm, weights_hbm, right_hbm, low_hbm,
-    tiles, basis_ref, left_ref, image_ref, away, near, other, zbuf, mc_ref, mr_ref,
+    n_row, n_col, est_hbm, dual_hbm, cov_hbm, basis_hbm, weights_ref, right_hbm, low_hbm, dual_tiles,
+    tiles, left_ref, image_ref, away, near, other, zbuf, mc_ref, mr_ref,
     gram, gram_terms, gram_part, gram_planes, gram_sum,
     inner, inner_terms, inner_part, inner_planes, inner_sum,
     inverse_ref, ritz_ref, iterate_ref, partner_ref,
@@ -185,15 +186,17 @@
 
     working = works(home, col)
     matrices = (est_hbm, dual_hbm, cov_hbm)
+    held = (tiles.at[0], dual_tiles, tiles.at[1])
 
     def load(which, step):
         there = flip(chip, chips - 1 - step // 2, chips)
         where = 2 * there + (1 - core + step) % 2
         columns = pl.ds(pl.multiple_of(where * piece, piece), piece)
         return pltpu.make_async_copy(
-            matrices[which].at[:, columns], tiles.at[which, where], load_sems.at[which, step]
+            matrices[which].at[:, columns], held[which].at[where], load_sems.at[which, step]
         )
 
+    basis_ref = image_ref.at[:, pl.ds(0, rank)]
     start_basis = pltpu.make_async_copy(basis_hbm, basis_ref, basis_sem)
     start_basis.start()
     for step in range(LOADS_AHEAD):
@@ -233,7 +236,7 @@
         where = 2 * flip(chip, chips - 1 - step // 2, chips) + (1 - core + step) % 2
 
         def product(which):
-            return jnp.dot(left_ref[...], tiles[which, where], preferred_element_type=jnp.float32)
+            return jnp.dot(left_ref[...], held[which][where], preferred_element_type=jnp.float32)
 
         both = penalty * (product(0) - product(1)) - product(2)
         return both[:rank] + both[rank:]
@@ -353,7 +356,7 @@
                     serve(col + hop, -1, k * (CHUNKS // 2) + part)
 
     image_ref[...] = jnp.zeros_like(image_ref)
-    strip = min(512, rows_tile)
+    strip = min(1024, rows_tile)
 
     def apply(where):
         upper, lower = split(mc_ref[where].T)
@@ -363,7 +366,7 @@
             rows = pl.ds(pl.multiple_of(index * strip, strip), strip)
 
             def product(which):
-                return jnp.dot(tiles[which, where, rows, :], right, preferred_element_type=jnp.float32)
+                return jnp.dot(held[which][where, rows, :], right, preferred_element_type=jnp.float32)
 
             image_ref[rows, :] += penalty * (product(0) - product(1)) - product(2)
             return carry
@@ -473,14 +476,16 @@
         upper, lower = split(mc_ref[k])
         tiles[0, k, :rank, :] = upper
         tiles[0, k, rank : 2 * rank, :] = upper
-        tiles[1, k, :rank, :] = lower
+        tiles[0, k, 2 * rank : 3 * rank, :] = lower
         return carry
 
     lax.fori_loop(0, n_row, prepare, 0)
     store_right = pltpu.make_async_copy(
         tiles.at[0, :, pl.ds(0, 2 * rank)], right_hbm, store_sems.at[0]
     )
-    store_low = pltpu.make_async_copy(tiles.at[1, :, pl.ds(0, rank)], low_hbm, store_sems.at[1])
+    store_low = pltpu.make_async_copy(
+        tiles.at[0, :, pl.ds(2 * rank, rank)], low_hbm, store_sems.at[1]
+    )
     store_right.start()
     store_low.start()
     inner_finish()
@@ -494,15 +499,13 @@
         wait_rows()
 
     for k in range(group):
-        tiles[2, 0, k * piece : (k + 1) * piece, : 2 * rank] = double(
+        weights_ref[k * piece : (k + 1) * piece, :] = double(
             fine_dot(mr_ref[k].T, partner_ref[...]), 1
         )
-    store_weights = pltpu.make_async_copy(
-        tiles.at[2, 0, :, pl.ds(0, 2 * rank)], weights_hbm, store_sems.at[2]
-    )
-    store_weights.start()
     gram_drain()
     inner_drain()
+    store_right.wait()
+    store_low.wait()
     for t in range(chips):
         to_sibling(t).wait_send()
         pair(t).wait_send()
@@ -532,10 +535,6 @@
                     @pl.when(target != row)
                     def _():
                         hop.wait_send()
-
-    store_right.wait()
-    store_low.wait()
-    store_weights.wait()
 
 
 def front(matrices, start_basis, n_row, n_col):
@@ -557,15 +556,15 @@
     return pl.pallas_call(
         functools.partial(front_kernel, n_row, n_col),
         in_specs=[pl.BlockSpec(memory_space=pl.ANY)] * 4,
-        out_specs=[pl.BlockSpec(memory_space=pl.ANY)] * 3,
+        out_specs=[VMEM] + [pl.BlockSpec(memory_space=pl.ANY)] * 2 + [VMEM],
         out_shape=(
-            jax.ShapeDtypeStruct((rows_tile, 2 * rank), jnp.bfloat16),
+            pltpu.VMEM((rows_tile, 2 * rank), jnp.bfloat16),
             jax.ShapeDtypeStruct((n_row, 2 * rank, piece), jnp.bfloat16),
             jax.ShapeDtypeStruct((n_row, rank, piece), jnp.bfloat16),
+            pltpu.VMEM((n_row, rows_tile, piece), jnp.bfloat16),
         ),
         scratch_shapes=[
-            pltpu.VMEM((3, n_row, rows_tile, piece), jnp.bfloat16),
-            pltpu.VMEM((rows_tile, rank), jnp.float32),
+            pltpu.VMEM((2, n_row, rows_tile, piece), jnp.bfloat16),
             pltpu.VMEM((2 * rank, rows_tile), jnp.bfloat16),
             pltpu.VMEM((rows_tile, 2 * rank), jnp.float32),
             pltpu.VMEM((chips, rank, piece), jnp.float32),
@@ -576,7 +575,7 @@
             pltpu.VMEM((group, rank, piece), jnp.float32),
             *sum_buffers, *sum_buffers,
             *[pltpu.VMEM((rank, rank), jnp.float32)] * 4,
-            dma((3, n_row)), dma, dma((3,)),
+            dma((3, n_row)), dma, dma((2,)),
             dma((chips,)), dma((chips,)),
             dma((chips - 1,)), dma((chips - 1,)),
             dma((chips - 1,)), dma((chips - 1,)),
@@ -586,7 +585,7 @@
             *sum_sems, *sum_sems,
         ],
         compiler_params=pltpu.CompilerParams(
-            collective_id=0, has_side_effects=True, vmem_limit_bytes=FULL_VMEM
+            collective_id=0, has_side_effects=True, vmem_limit_bytes=FRONT_VMEM
         ),
     )(*matrices, start_basis)
 
@@ -703,7 +702,8 @@
 def finish_kernel(weights_ref, right_ref, low_ref, dual_ref, est_ref, clip_ref):
     step = pl.program_id(0)
     count, rank, piece = low_ref.shape
-    depth = dual_ref.shape[0]
+    depth = est_ref.shape[0]
+    lines = pl.ds(pl.multiple_of(step * depth, depth), depth)
     n_grid = pl.num_programs(0)
     row_start = (lax.axis_index("row") * n_grid + step) * depth
     gap = (
@@ -713,45 +713,50 @@
     for k in range(count):
         where = slice(k * piece, (k + 1) * piece)
         col_start = lax.axis_index("col") * (count * piece) + k * piece
-        theta = jnp.dot(weights_ref[...], right_ref[k], preferred_element_type=jnp.float32)
-        theta += jnp.dot(weights_ref[:, :rank], low_ref[k], preferred_element_type=jnp.float32)
+        theta = jnp.dot(weights_ref[lines, :], right_ref[k], preferred_element_type=jnp.float32)
+        theta += jnp.dot(weights_ref[lines, :rank], low_ref[k], preferred_element_type=jnp.float32)
         theta += jnp.where(gap == row_start - col_start, base_level, 0.0)
-        mixture = theta + dual_ref[:, where].astype(jnp.float32)
+        mixture = theta + dual_ref[k, lines, :].astype(jnp.float32)
         clipped = jnp.clip(mixture, -threshold, threshold)
         est_ref[:, where] = mixture - clipped
         clip_ref[:, where] = clipped.astype(jnp.bfloat16)
 
 
-def finish(weights, right, low, dual_var):
-    rows_tile, cols_tile = dual_var.shape
+def near_by(value):
+    return pltpu.with_memory_space_constraint(value, pltpu.VMEM)
+
+
+def finish(weights, right, low, dual_tiles):
+    count, rows_tile, piece = dual_tiles.shape
+    whole = (rows_tile, count * piece)
+    cols_tile = whole[1]
     depth = min(FINISH_ROWS, rows_tile)
     wide = pl.BlockSpec((depth, cols_tile), lambda step: (step, 0))
     return pl.pallas_call(
         finish_kernel,
         grid=(rows_tile // depth,),
         in_specs=[
-            pl.BlockSpec((depth, weights.shape[1]), lambda step: (step, 0)),
+            VMEM,
             pl.BlockSpec(right.shape, lambda step: (0, 0, 0)),
             pl.BlockSpec(low.shape, lambda step: (0, 0, 0)),
-            wide,
+            VMEM,
         ],
         out_specs=(wide, wide),
         out_shape=(
-            jax.ShapeDtypeStruct(dual_var.shape, jnp.float32),
-            jax.ShapeDtypeStruct(dual_var.shape, jnp.bfloat16),
+            jax.ShapeDtypeStruct(whole, jnp.float32),
+            jax.ShapeDtypeStruct(whole, jnp.bfloat16),
         ),
         compiler_params=pltpu.CompilerParams(
             dimension_semantics=("arbitrary",), vmem_limit_bytes=VMEM_BYTES
         ),
-    )(weights, right, low, dual_var)
+    )(near_by(weights), right, low, near_by(dual_tiles))
 
 
 def fast_body(n_row, n_col, covariance, estimate, dual_var, start_basis):
     rows_tile, cols_tile = covariance.shape
     rank = start_basis.shape[1]
     matrices = (estimate, dual_var, covariance)
-    weights, right, low = front(matrices, start_basis, n_row, n_col)
-    return finish(weights, right, low, dual_var)
+    return finish(*front(matrices, start_basis, n_row, n_col))
 
 
 def body(covariance, estimate, dual_var, start_basis):
@@ -767,12 +772,12 @@
         and rows_tile % piece == 0
         and rank % 128 == 0
         and rank % (8 * n_row) == 0
-        and 2 * rank <= min(rows_tile, piece)
+        and 3 * rank <= min(rows_tile, piece)
         and n_row & (n_row - 1) == 0
         and n_row >= max(8, 2 * n_col)
         and rank % (8 * CHUNKS) == 0
         and n_row > LOADS_AHEAD
-        and 6 * rows_tile * cols_tile + 19 * rank * cols_tile <= FULL_VMEM
+        and 6 * rows_tile * cols_tile + 23 * rank * cols_tile <= FULL_VMEM
     )
     if not fits:
         return plain_body(covariance, estimate, dual_var, start_basis)

time: 110 us -> 100 us (0.909)
  Pallas kernels: 109 us -> 99.3 us
    pallas_call x1, Pallas kernels: 24.6 us -> 19.7 us  [finish(): pl.pallas_call(finish_kernel, grid=(rows_tile // depth,), in_specs=[VMEM,...]
    pallas_call x1, Pallas kernels: 84.5 us -> 79.7 us  [front(): pl.pallas_call(functools.partial(front_kernel, n_row, n_col), in_specs=[p...]
where the time goes in v3:
time: 100 us
  Pallas kernels  99.3 us (99%)
    pallas_call x1, Pallas kernels, front(): pl.pallas_call(functools.partial(front_kernel, n_row, n_col), in_specs=[p...  79.7 us
    pallas_call x1, Pallas kernels, finish(): pl.pallas_call(finish_kernel, grid=(rows_tile // depth,), in_specs=[VMEM,...  19.7 us

profile of v3, /device:TPU:0, one launch (start us, length us, event | category | flops | bytes accessed | tf_op | source)
XLA Modules:
  0.0 100.0 jit_solution(2819331986382015207)
XLA Ops:
  0.6 79.7 %shard_map.59 = (bf16[2048,256]{1,0:T(8,128)(2,1)S(1)}, bf16[8,256,512]{2,1,0:T(8,128)(2,1)}, bf16[8,128,512]{2,1,0:T(8,128)(2,1)}, bf16[8,2048,512]{2,1,0:T(8,128)(2,1)S(1)}) custom-call(bf16[2048,4096]{1,0:T(8,128)(2,1)} %est_hbm.1, bf16[2048,4096]{1,0:T(8,128)(2,1)} %dual_hbm.1, bf16[2048,4096]{1,0:T(8,128)(2,1)} %cov_hbm.1, f32[2048,128]{1,0:T(8,128)} %basis_hbm.1), custom_call_target="tpu_custom_call" | custom-call | tf_op jit(solution)/shard_map/pallas_call | solution.py:556
  80.3 19.7 %shard_map.60 = (f32[2048,4096]{1,0:T(8,128)}, bf16[2048,4096]{1,0:T(8,128)(2,1)}) custom-call(bf16[2048,256]{1,0:T(8,128)(2,1)S(1)} %get-tuple-element.6.weights_ref, bf16[8,256,512]{2,1,0:T(8,128)(2,1)} %get-tuple-element.7.right_ref, bf16[8,128,512]{2,1,0:T(8,128)(2,1)} %get-tuple-element.8.low_ref, bf16[8,2048,512]{2,1,0:T(8,128)(2,1)S(1)} %get-tuple-element.9.dual_ref), custom_call_target="tpu_custom_call" | custom-call | tf_op jit(solution)/shard_map/pallas_call | solution.py:735
